TPU v7x, 32 devices: a whole 2x2x4 slice. The times are simulated.
32 devices in a mesh: parts: 2 (over y), seq: 4 (over z), head: 2 (over x), rep: 2 (over core).
Axes of the slice: x: 2, y: 2, z: 4, core: 2. Of those that a mesh axis runs over, the one named last changes fastest.
Arguments:
- queries: bfloat16 [4, 1024, 2048], P(('parts', 'rep'), 'seq', 'head'), parts along dimension 0, may hold values from -6 to 6
- reflect_keys: bfloat16 [4, 1024, 2, 2048], P(('parts', 'rep'), 'seq', None, 'head'), parts along dimension 0, may hold values from -6 to 6
- reflect_values: bfloat16 [4, 1024, 2, 2048], P(('parts', 'rep'), 'seq', None, 'head'), parts along dimension 0, may hold values from -6 to 6
- reflect_beta: float32 [4, 1024, 2, 16], P(('parts', 'rep'), 'seq', None, 'head'), parts along dimension 0, may hold values from 0.2 to 2
- log_decay: float32 [4, 1024, 16], P(('parts', 'rep'), 'seq', 'head'), parts along dimension 0, may hold values from -2.5 to 0
- prompt_lengths: int32 [4, 6], P(('parts', 'rep')), parts along dimension 0, may hold values from 1 to 512, 1024 in all within a row
- norm_gain: float32 [128], replicated, may hold values from 0.1 to 1.9
- out_weight: bfloat16 [2048, 2048], P('head'), may hold values from -0.125 to 0.125
Outputs:
- layer_out: bfloat16 [4, 1024, 2048], P(('parts', 'rep'), ('seq', 'head')), parts along dimension 0
There are 2 independent parts, one for each index of `parts`. A program takes and returns all parts, laid end to end along the dimension named above; an argument that names none is the same for every part. Nothing has to cross between parts.
Inputs may be any that keep to these rules, and one draw needn't show every extreme that they name: `prompt_lengths`: the 6 prompts of a pack lie end to end from its first token and cover all 1024 tokens; the longest has exactly 512.
All inputs are finite; a program needn't handle non-finite values.
Results may differ from a plain program's by a relative error of at most 0.0095.
Values may be sent and summed in bfloat16 or wider, within the bound.
A program may use at most 64 MiB of HBM per device.

v0:
```python
import functools

import jax
import jax.numpy as jnp
from jax import lax
from jax.experimental import pallas as pl
from jax.experimental.pallas import tpu as pltpu
from jax.sharding import PartitionSpec as P

BLOCK = 64
HEADS_STEP = 2

epsilon = 1e-06
f32 = jnp.float32
bf16 = jnp.bfloat16
highest = lax.Precision.HIGHEST


def mm(a, b):
    return jnp.dot(a, b, preferred_element_type=f32)


def mm_nt(a, b):
    return lax.dot_general(a, b, (((1,), (1,)), ((), ())), preferred_element_type=f32)


def mm_tn(a, b, precision=None):
    return lax.dot_general(
        a, b, (((0,), (0,)), ((), ())), preferred_element_type=f32, precision=precision
    )


def split(x):
    hi = x.astype(bf16)
    return hi, (x - hi.astype(f32)).astype(bf16)


def local_kernel(
    refl, blocks, len_ref, q_ref, k_ref, v_ref, beta_ref, gate_ref,
    oloc_ref, read_ref, add_ref, map_ref, rows_ref,
):
    sub = refl * BLOCK
    width = k_ref.shape[1] // HEADS_STEP
    heads = gate_ref.shape[1]
    tokens = blocks * BLOCK
    step = pl.program_id(0)

    @pl.when(step == 0)
    def _():
        tok = lax.broadcasted_iota(jnp.int32, (tokens, sub), 0)
        lane = lax.broadcasted_iota(jnp.int32, (tokens, sub), 1)
        for b in range(blocks):
            rel = tok - b * BLOCK
            cum = jnp.where((rel >= 0) & (rel <= lane // refl), 1.0, 0.0).astype(f32)
            rows_ref[b, 0] = mm_tn(gate_ref[...], cum, highest)
            total = jnp.zeros((heads, sub), f32)
            for j in range(refl):
                pick = jnp.where(rel * refl + j == lane, 1.0, 0.0).astype(f32)
                pick = jnp.where(rel >= 0, pick, 0.0)
                total += mm_tn(beta_ref[:, j * heads : (j + 1) * heads], pick, highest)
            rows_ref[b, 1] = total

    offset = lax.axis_index("seq") * tokens
    ends = []
    running = 0
    for d in range(len_ref.shape[1]):
        running = running + len_ref[0, d]
        ends.append(running)

    def segment(pos):
        total = jnp.zeros(pos.shape, jnp.int32)
        for end in ends:
            total += jnp.where(pos >= end, 1, 0)
        return total

    row_i = lax.broadcasted_iota(jnp.int32, (sub, sub), 0)
    col_i = lax.broadcasted_iota(jnp.int32, (sub, sub), 1)
    eye = row_i == col_i
    eye_f = jnp.where(eye, 1.0, 0.0).astype(f32)
    tok_i = lax.broadcasted_iota(jnp.int32, (BLOCK, sub), 0)
    tok_j = lax.broadcasted_iota(jnp.int32, (BLOCK, sub), 1)
    pick_tok = tok_j == tok_i * refl + refl - 1
    levels = []
    size = refl
    while size < sub:
        big = min(4 * size, sub)
        levels.append((row_i // big == col_i // big) & (row_i // size > col_i // size))
        size = big

    blocks_geo = []
    for b in range(blocks):
        start = offset + b * BLOCK
        seg_row = segment(start + lax.broadcasted_iota(jnp.int32, (1, sub), 1) // refl)
        seg_col = segment(start + lax.broadcasted_iota(jnp.int32, (sub, 1), 0) // refl)
        seg_tok = segment(start + lax.broadcasted_iota(jnp.int32, (BLOCK, 1), 0))
        before = jnp.where(start == 0, -1, 0)
        last_seg = 0
        for end in ends:
            before += jnp.where(start - 1 >= end, 1, 0)
            last_seg += jnp.where(start + BLOCK - 1 >= end, 1, 0)
        incl = (row_i >= col_i) & (seg_col == seg_row)
        read = (tok_j // refl <= tok_i) & (seg_tok == seg_row)
        blocks_geo.append(
            (incl, read, seg_row == before, seg_tok == before, seg_col == last_seg, last_seg == before)
        )

    for h in range(HEADS_STEP):
        cols = slice(h * width, (h + 1) * width)
        head = step * HEADS_STEP + h
        state = None
        for b in range(blocks):
            incl, read, carry_on, tok_on, end_on, all_on = blocks_geo[b]
            kb = k_ref[b * sub : (b + 1) * sub, cols]
            vb = v_ref[b * sub : (b + 1) * sub, cols]
            qb = q_ref[b * BLOCK : (b + 1) * BLOCK, cols]
            c_row = rows_ref[b, 0, pl.ds(head, 1), :]
            beta_row = rows_ref[b, 1, pl.ds(head, 1), :]
            gram = mm_nt(kb, kb)
            diag = jnp.where(eye, gram, 0.0)
            n_row = lax.rsqrt(jnp.sum(diag, axis=0, keepdims=True) + epsilon)
            n_col = lax.rsqrt(jnp.sum(diag, axis=1, keepdims=True) + epsilon)
            c_col = jnp.sum(jnp.where(eye, c_row, 0.0), axis=1, keepdims=True)
            beta_col = jnp.sum(jnp.where(eye, beta_row, 0.0), axis=1, keepdims=True)
            ratio = jnp.where(incl, jnp.exp(jnp.minimum(c_col - c_row, 0.0)), 0.0)
            low = jnp.where(eye, 0.0, (beta_col * n_col) * ratio * gram * n_row)
            inv = eye_f - jnp.where(row_i // refl == col_i // refl, low, 0.0)
            for mask in levels:
                inv_b = inv.astype(bf16)
                nil = mm(inv_b, jnp.where(mask, low, 0.0).astype(bf16)).astype(bf16)
                both = mm(nil, jnp.concatenate([nil, inv_b], axis=1))
                half = inv - both[:, sub:]
                inv = half + mm(both[:, :sub].astype(bf16), half.astype(bf16))
            inv_b = inv.astype(bf16)
            low_hi, low_lo = split(low)
            resid = eye_f - inv_b.astype(f32) - mm(
                jnp.concatenate([low_hi, low_lo], axis=1), jnp.concatenate([inv_b, inv_b], axis=0)
            )
            inv = inv_b.astype(f32) + mm(inv_b, resid.astype(bf16))
            carry_row = jnp.where(carry_on, jnp.exp(c_row), 0.0)
            tv = jnp.concatenate(split(inv * beta_row), axis=1)
            tk = jnp.concatenate(split(inv * (beta_row * carry_row * n_row)), axis=1)
            kk = jnp.concatenate([kb, kb], axis=0)
            writes = jnp.concatenate([mm(tv, jnp.concatenate([vb, vb], axis=0)), mm(tk, kk)], axis=1)
            c_end = c_row[:, sub - 1 : sub]
            e_col = jnp.where(end_on, jnp.exp(jnp.minimum(c_end - c_col, 0.0)), 0.0) * n_col
            ends_w = jnp.concatenate(split(writes * e_col), axis=0)
            step_w = mm_tn(kk, ends_w)
            carry_end = jnp.where(all_on, jnp.exp(c_end), 0.0)
            block_map = carry_end * eye_f - step_w[:, width:]
            block_add = step_w[:, :width]
            qf = qb.astype(f32)
            nq = lax.rsqrt(jnp.sum(qf * qf, axis=1, keepdims=True) + epsilon) * width ** (-0.5)
            ct = jnp.sum(jnp.where(pick_tok, c_row, 0.0), axis=1, keepdims=True)
            weights = (
                jnp.where(read, jnp.exp(jnp.minimum(ct - c_row, 0.0)), 0.0)
                * mm_nt(qb, kb) * nq * n_row
            )
            reads = mm(weights.astype(bf16), writes.astype(bf16))
            own = reads[:, :width]
            back = (jnp.where(tok_on, jnp.exp(ct), 0.0) * nq) * qf - reads[:, width:]
            if state is None:
                state = jnp.concatenate([block_add, block_map], axis=1)
                out_own, out_back = own, back
            else:
                s_hi, s_lo = split(state)
                m_hi, m_lo = split(block_map)
                moved = mm(back.astype(bf16), s_hi)
                out_own, out_back = own + moved[:, :width], moved[:, width:]
                state = mm(
                    jnp.concatenate([m_hi, m_lo], axis=1), jnp.concatenate([s_hi, s_hi], axis=0)
                ) + mm(m_hi, s_lo)
                state = jnp.concatenate([state[:, :width] + block_add, state[:, width:]], axis=1)
            oloc_ref[b * BLOCK : (b + 1) * BLOCK, cols] = out_own
            read_ref[b * BLOCK : (b + 1) * BLOCK, cols] = out_back.astype(bf16)
        add_ref[h] = state[:, :width]
        map_ref[h] = state[:, width:]


def local_part(lengths, q, k, v, beta, gate):
    tokens, heads = gate.shape
    refl = k.shape[0] // tokens
    width = q.shape[1] // heads
    blocks = tokens // BLOCK
    wide = HEADS_STEP * width
    whole = lambda *shape: pl.BlockSpec(shape, lambda i: (0,) * len(shape))
    column = lambda rows: pl.BlockSpec((rows, wide), lambda i: (0, i))
    square = pl.BlockSpec((HEADS_STEP, width, width), lambda i: (i, 0, 0))
    return pl.pallas_call(
        functools.partial(local_kernel, refl, blocks),
        grid=(heads // HEADS_STEP,),
        in_specs=[
            pl.BlockSpec(memory_space=pltpu.SMEM),
            column(tokens), column(tokens * refl), column(tokens * refl),
            whole(*beta.shape), whole(*gate.shape),
        ],
        out_specs=[column(tokens), column(tokens), square, square],
        out_shape=[
            jax.ShapeDtypeStruct(q.shape, f32),
            jax.ShapeDtypeStruct(q.shape, bf16),
            jax.ShapeDtypeStruct((heads, width, width), f32),
            jax.ShapeDtypeStruct((heads, width, width), f32),
        ],
        scratch_shapes=[pltpu.VMEM((blocks, 2, heads, refl * BLOCK), f32)],
        compiler_params=pltpu.CompilerParams(vmem_limit_bytes=48 * 2**20),
    )(lengths, q, k, v, beta, gate)


def body(queries, reflect_keys, reflect_values, reflect_beta, log_decay, prompt_lengths, norm_gain, out_weight):
    tokens, refl, wide = reflect_keys.shape[1:]
    heads = log_decay.shape[2]
    width = wide // heads
    count = lax.axis_size("seq")
    oloc, read, add, maps = local_part(
        prompt_lengths,
        queries[0],
        reflect_keys[0].reshape(tokens * refl, wide),
        reflect_values[0].reshape(tokens * refl, wide),
        reflect_beta[0].reshape(tokens, refl * heads),
        log_decay[0],
    )
    state = jnp.zeros((heads, width, width), bf16)
    maps_b = maps.astype(bf16)
    for hop in range(count - 1):
        grown = jnp.einsum("hij,hjk->hik", maps_b, state, preferred_element_type=f32) + add
        state = lax.ppermute(grown.astype(bf16), "seq", [(s, s + 1) for s in range(count - 1)])
    out = oloc.reshape(tokens, heads, width) + jnp.einsum(
        "thk,hkv->thv", read.reshape(tokens, heads, width), state, preferred_element_type=f32
    )
    normed = (
        out * lax.rsqrt(jnp.mean(out * out, axis=-1, keepdims=True) + epsilon) * norm_gain
    ).astype(bf16)
    partial = jnp.dot(normed.reshape(tokens, wide), out_weight, preferred_element_type=f32).astype(bf16)
    return lax.psum_scatter(partial, "head", scatter_dimension=0, tiled=True)[None]


def solution(mesh):
    in_specs = (
        P(("parts", "rep"), "seq", "head"),
        P(("parts", "rep"), "seq", None, "head"),
        P(("parts", "rep"), "seq", None, "head"),
        P(("parts", "rep"), "seq", None, "head"),
        P(("parts", "rep"), "seq", "head"),
        P(("parts", "rep"), None),
        P(),
        P("head", None),
    )
    out_specs = P(("parts", "rep"), ("seq", "head"), None)
    return jax.shard_map(body, mesh=mesh, in_specs=in_specs, out_specs=out_specs, check_vma=False)
```

profile of v0, /device:TPU:28, one launch (start us, length us, event | category | flops | bytes accessed | tf_op | source)
XLA Modules:
  0.0 140.1 jit_solution(12783561863899448557)
XLA Ops:
  6.5 0.8 copy.15.beta_ref
  7.4 0.8 copy.14
  8.2 1.5 %reshape_squeeze.9.k_ref = bf16[512,1024]{1,0:T(8,128)(2,1)S(1)} reshape(bf16[1,256,2,1024]{3,2,1,0:T(2,128)(2,1)} %param.9) | data formatting | bytes 2097152 | tf_op jit(solution)/shard_map/reshape;squeeze | solution.py:216
  9.7 1.5 %reshape_squeeze.10.v_ref = bf16[512,1024]{1,0:T(8,128)(2,1)S(1)} reshape(bf16[1,256,2,1024]{3,2,1,0:T(2,128)(2,1)} %param.10) | data formatting | bytes 2097152 | tf_op jit(solution)/shard_map/reshape;squeeze | solution.py:217
  11.2 0.0 copy-start
  11.2 1.0 copy-done
  12.2 67.8 %shard_map.82 = (f32[256,1024]{1,0:T(8,128)S(1)}, bf16[256,1024]{1,0:T(8,128)(2,1)S(1)}, f32[8,128,128]{2,1,0:T(8,128)S(1)}, f32[8,128,128]{2,1,0:T(8,128)S(1)}) custom-call(s32[1,6]{1,0:T(1,128)S(1)} %copy-done.2, bf16[256,1024]{1,0:T(8,128)(2,1)S(1)} %bitcast.25, bf16[512,1024]{1,0:T(8,128)(2,1)S(1)} %reshape_squeeze.9.k_ref, ...), custom_call_target="tpu_custom_call" | custom-call | tf_op jit(solution)/shard_map/pallas_call | solution.py:188
  80.0 0.0 copy-start.1
  80.0 0.2 fusion.1
  80.2 0.0 copy-start.3
  80.2 1.3 collective-permute-start
  81.5 8.6 %collective-permute-done = bf16[8,128,128]{2,1,0:T(8,128)(2,1)S(1)} collective-permute-done((bf16[8,128,128]{2,1,0:T(8,128)(2,1)S(1)}, bf16[8,128,128]{2,1,0:T(8,128)(2,1)S(1)}, u32[]{:S(2)}, u32[]{:S(2)}) %collective-permute-start) | collective-permute-done | bytes 262176 | tf_op jit(solution)/shard_map/ppermute | solution.py:225
  90.2 0.2 fusion.2
  90.4 1.3 collective-permute-start.1
  91.7 7.8 %collective-permute-done.1 = bf16[8,128,128]{2,1,0:T(8,128)(2,1)S(1)} collective-permute-done((bf16[8,128,128]{2,1,0:T(8,128)(2,1)S(1)}, bf16[8,128,128]{2,1,0:T(8,128)(2,1)S(1)}, u32[]{:S(2)}, u32[]{:S(2)}) %collective-permute-start.1) | collective-permute-done | bytes 262176 | tf_op jit(solution)/shard_map/ppermute | solution.py:225
  99.5 0.2 fusion.3
  99.7 1.3 collective-permute-start.2
  101.0 0.3 copy.20
  101.4 6.6 %collective-permute-done.2 = bf16[8,128,128]{2,1,0:T(8,128)(2,1)S(1)} collective-permute-done((bf16[8,128,128]{2,1,0:T(8,128)(2,1)S(1)}, bf16[8,128,128]{2,1,0:T(8,128)(2,1)S(1)}, u32[]{:S(2)}, u32[]{:S(2)}) %collective-permute-start.2) | collective-permute-done | bytes 262176 | tf_op jit(solution)/shard_map/ppermute | solution.py:225
  108.0 1.4 multiply_reduce_fusion
  109.4 0.1 multiply_convert_fusion
  109.5 2.2 %convolution_convert_fusion = bf16[256,2048]{1,0:T(8,128)(2,1)} fusion(bf16[256,1024]{0,1:T(8,128)(2,1)S(1)} %bitcast.27, bf16[1024,2048]{1,0:T(8,128)(2,1)S(1)} %copy-done.4), kind=kOutput, calls=%fused_computation | convolution fusion | flops 1074266112 | bytes 5767168 | tf_op jit(solution)/shard_map/dot_general | solution.py:232
  111.8 0.0 reduce-scatter.2.cloned.1.call-update
  111.8 21.5 %reduce-scatter.2.cloned.1.call-done = bf16[128,2048]{1,0:T(8,128)(2,1)} async-done(((bf16[256,2048]{1,0:T(8,128)(2,1)}), bf16[128,2048]{1,0:T(8,128)(2,1)}) %reduce-scatter.2.cloned.1.call-update) | async-done | bytes 524304 | tf_op jit(solution)/shard_map/reduce_scatter | solution.py:233
  (8 shorter events, 0.0 us)
Async XLA Ops:
  6.5 4.6 %copy-start.2 = (s32[1,6]{1,0:T(1,128)S(1)}, s32[1,6]{1,0:T(1,128)}, u32[]{:S(2)}) copy-start(s32[1,6]{1,0:T(1,128)} %len_ref.1) | copy-start | bytes 76
  6.5 126.7 %reduce-scatter.2.cloned.1.call-start = ((), (), s32[]{:S(2)}) async-start(), calls=%async_computation.1 | async-start | bytes 1572864 | tf_op jit(solution)/shard_map/reduce_scatter | solution.py:233
  11.2 1.0 copy-start
  80.0 19.7 %copy-start.1 = (bf16[256,1024]{1,0:T(8,128)(2,1)}, bf16[256,1024]{1,0:T(8,128)(2,1)S(1)}, u32[]{:S(2)}) copy-start(bf16[256,1024]{1,0:T(8,128)(2,1)S(1)} %get-tuple-element.12) | copy-start | bytes 1572868
  80.2 29.2 %copy-start.3 = (f32[128]{0:T(128)S(1)}, f32[128]{0:T(128)}, u32[]{:S(2)}) copy-start(f32[128]{0:T(128)} %param.14) | copy-start | bytes 1540
  80.2 9.9 %collective-permute-start = (bf16[8,128,128]{2,1,0:T(8,128)(2,1)S(1)}, bf16[8,128,128]{2,1,0:T(8,128)(2,1)S(1)}, u32[]{:S(2)}, u32[]{:S(2)}) collective-permute-start(bf16[8,128,128]{2,1,0:T(8,128)(2,1)S(1)} %fusion.1), channel_id=1, source_target_pairs={{0,4},{4,8},{8,12},{1,5},{5,9},{9,13},{2,6},{6,10},{10,14},{3,7},{... | collective-permute-start | bytes 786440 | tf_op jit(solution)/shard_map/ppermute | solution.py:225
  90.4 9.1 %collective-permute-start.1 = (bf16[8,128,128]{2,1,0:T(8,128)(2,1)S(1)}, bf16[8,128,128]{2,1,0:T(8,128)(2,1)S(1)}, u32[]{:S(2)}, u32[]{:S(2)}) collective-permute-start(bf16[8,128,128]{2,1,0:T(8,128)(2,1)S(1)} %fusion.2), channel_id=1, source_target_pairs={{0,4},{4,8},{8,12},{1,5},{5,9},{9,13},{2,6},{6,10},{10,14},{3,7},{... | collective-permute-start | bytes 786440 | tf_op jit(solution)/shard_map/ppermute | solution.py:225
  99.7 8.3 %collective-permute-start.2 = (bf16[8,128,128]{2,1,0:T(8,128)(2,1)S(1)}, bf16[8,128,128]{2,1,0:T(8,128)(2,1)S(1)}, u32[]{:S(2)}, u32[]{:S(2)}) collective-permute-start(bf16[8,128,128]{2,1,0:T(8,128)(2,1)S(1)} %fusion.3), channel_id=1, source_target_pairs={{0,4},{4,8},{8,12},{1,5},{5,9},{9,13},{2,6},{6,10},{10,14},{3,7},{... | collective-permute-start | bytes 786440 | tf_op jit(solution)/shard_map/ppermute | solution.py:225
  101.3 8.2 %copy-start.4 = (bf16[1024,2048]{1,0:T(8,128)(2,1)S(1)}, bf16[1024,2048]{1,0:T(8,128)(2,1)}, u32[]{:S(2)}) copy-start(bf16[1024,2048]{1,0:T(8,128)(2,1)} %param.15) | copy-start | bytes 12582916
Sparse Core Ops, SparseCore 0:
  111.9 21.2 reduce-scatter.1
where the time goes:
time: 142 us; the launch traced here: 140 us
  Pallas kernels  67.8 us (48%)
  waiting for transfers between devices  44.5 us (31%)
  between operations  13.6 us (10%)
  local copies, waits for them, and re-layouts  5.98 us (4%)
  matrix products  4.28 us (3%)
  starting transfers between devices  3.88 us (3%)
    pallas_call x1, Pallas kernels, local_part(): pl.pallas_call(functools.partial(local_kernel, refl, blocks), grid=(heads...  67.8 us
    ppermute x3, waiting for transfers between devices, body(): lax.ppermute(grown.astype(bf16), 'seq', [(s, s + 1) for s in range(count...  23 us
    reduce_scatter x1, waiting for transfers between devices, body(): lax.psum_scatter(partial, 'head', scatter_dimension=0, tiled=True)[None]  21.5 us
    ppermute x3, starting transfers between devices, body(): lax.ppermute(grown.astype(bf16), 'seq', [(s, s + 1) for s in range(count...  3.88 us
  transfers between devices with their start and end apart: 4, of which 4 were waited for; matrix products, arithmetic and copies ran while one was open for 0% of the time, Pallas kernels for 0%

commit v1 on v0

v1 whole, which is shorter than its diff:
```python
import functools

import jax
import jax.numpy as jnp
from jax import lax
from jax.experimental import pallas as pl
from jax.experimental.pallas import tpu as pltpu
from jax.sharding import PartitionSpec as P

BLOCK = 64
HEADS_STEP = 4
STATE_GROUP = 2
PIECES = 4
MESH = pl.DeviceIdType.MESH

epsilon = 1e-06
f32 = jnp.float32
bf16 = jnp.bfloat16
highest = lax.Precision.HIGHEST


def mm(a, b):
    return jnp.dot(a, b, preferred_element_type=f32)


def mm_nt(a, b):
    return lax.dot_general(a, b, (((1,), (1,)), ((), ())), preferred_element_type=f32)


def mm_tn(a, b, precision=None):
    return lax.dot_general(
        a, b, (((0,), (0,)), ((), ())), preferred_element_type=f32, precision=precision
    )


def split(x):
    hi = x.astype(bf16)
    return hi, (x - hi.astype(f32)).astype(bf16)


def local_kernel(
    refl, blocks, len_ref, q_ref, k_ref, v_ref, beta_ref, gate_ref,
    oloc_ref, read_ref, add_ref, map_ref, rows_ref,
):
    sub = refl * BLOCK
    width = k_ref.shape[1] // HEADS_STEP
    heads = gate_ref.shape[1]
    tokens = blocks * BLOCK
    step = pl.program_id(0)

    @pl.when(step == 0)
    def _():
        tok = lax.broadcasted_iota(jnp.int32, (tokens, sub), 0)
        lane = lax.broadcasted_iota(jnp.int32, (tokens, sub), 1)
        for b in range(blocks):
            rel = tok - b * BLOCK
            cum = jnp.where((rel >= 0) & (rel <= lane // refl), 1.0, 0.0).astype(f32)
            rows_ref[b, 0] = mm_tn(gate_ref[...], cum, highest)
            total = jnp.zeros((heads, sub), f32)
            for j in range(refl):
                pick = jnp.where(rel * refl + j == lane, 1.0, 0.0).astype(f32)
                pick = jnp.where(rel >= 0, pick, 0.0)
                total += mm_tn(beta_ref[:, j * heads : (j + 1) * heads], pick, highest)
            rows_ref[b, 1] = total

    offset = lax.axis_index("seq") * tokens
    ends = []
    running = 0
    for d in range(len_ref.shape[1]):
        running = running + len_ref[0, d]
        ends.append(running)

    def segment(pos):
        total = jnp.zeros(pos.shape, jnp.int32)
        for end in ends:
            total += jnp.where(pos >= end, 1, 0)
        return total

    row_i = lax.broadcasted_iota(jnp.int32, (sub, sub), 0)
    col_i = lax.broadcasted_iota(jnp.int32, (sub, sub), 1)
    eye = row_i == col_i
    eye_f = jnp.where(eye, 1.0, 0.0).astype(f32)
    tok_i = lax.broadcasted_iota(jnp.int32, (BLOCK, sub), 0)
    tok_j = lax.broadcasted_iota(jnp.int32, (BLOCK, sub), 1)
    pick_tok = tok_j == tok_i * refl + refl - 1
    levels = []
    size = refl
    while size < sub:
        big = min(4 * size, sub)
        levels.append((row_i // big == col_i // big) & (row_i // size > col_i // size))
        size = big

    blocks_geo = []
    for b in range(blocks):
        start = offset + b * BLOCK
        seg_row = segment(start + lax.broadcasted_iota(jnp.int32, (1, sub), 1) // refl)
        seg_col = segment(start + lax.broadcasted_iota(jnp.int32, (sub, 1), 0) // refl)
        seg_tok = segment(start + lax.broadcasted_iota(jnp.int32, (BLOCK, 1), 0))
        before = jnp.where(start == 0, -1, 0)
        last_seg = 0
        for end in ends:
            before += jnp.where(start - 1 >= end, 1, 0)
            last_seg += jnp.where(start + BLOCK - 1 >= end, 1, 0)
        incl = (row_i >= col_i) & (seg_col == seg_row)
        read = (tok_j // refl <= tok_i) & (seg_tok == seg_row)
        blocks_geo.append(
            (incl, read, seg_row == before, seg_tok == before, seg_col == last_seg, last_seg == before)
        )

    pairs = [(h, b) for h in range(HEADS_STEP) for b in range(blocks)]

    def over(stage, *lists):
        return [stage(h, b, *args) for (h, b), *args in zip(pairs, *lists)]

    def cols(h):
        return slice(h * width, (h + 1) * width)

    def keys(h, b):
        return k_ref[b * sub : (b + 1) * sub, cols(h)]

    def row(kind, h, b):
        return rows_ref[b, kind, pl.ds(step * HEADS_STEP + h, 1), :]

    def column(values):
        return jnp.sum(jnp.where(eye, values, 0.0), axis=1, keepdims=True)

    def scales(h, b):
        gram = mm_nt(keys(h, b), keys(h, b))
        diag = jnp.where(eye, gram, 0.0)
        n_row = lax.rsqrt(jnp.sum(diag, axis=0, keepdims=True) + epsilon)
        n_col = lax.rsqrt(jnp.sum(diag, axis=1, keepdims=True) + epsilon)
        c_row = row(0, h, b)
        c_col = column(c_row)
        ratio = jnp.where(blocks_geo[b][0], jnp.exp(jnp.minimum(c_col - c_row, 0.0)), 0.0)
        low = jnp.where(eye, 0.0, (column(row(1, h, b)) * n_col) * ratio * gram * n_row)
        return low, n_row, n_col, c_col

    lows, n_rows, n_cols, c_cols = zip(*over(scales))
    invs = [eye_f - jnp.where(row_i // refl == col_i // refl, low, 0.0) for low in lows]
    for mask in levels:
        heads_b = [inv.astype(bf16) for inv in invs]
        nils = [
            mm(inv, jnp.where(mask, low, 0.0).astype(bf16)).astype(bf16)
            for inv, low in zip(heads_b, lows)
        ]
        both = [mm(nil, jnp.concatenate([nil, inv], axis=1)) for nil, inv in zip(nils, heads_b)]
        halves = [inv - pair[:, sub:] for inv, pair in zip(invs, both)]
        invs = [
            half + mm(pair[:, :sub].astype(bf16), half.astype(bf16))
            for half, pair in zip(halves, both)
        ]

    def residual(h, b, inv, low):
        inv_b = inv.astype(bf16)
        low_2 = jnp.concatenate(split(low), axis=1)
        return eye_f - inv_b.astype(f32) - mm(low_2, jnp.concatenate([inv_b, inv_b], axis=0))

    resids = over(residual, invs, lows)

    def refine(h, b, inv, resid):
        inv_b = inv.astype(bf16)
        return inv_b.astype(f32) + mm(inv_b, resid.astype(bf16))

    invs = over(refine, invs, resids)

    def write(h, b, inv, n_row):
        carry_row = jnp.where(blocks_geo[b][2], jnp.exp(row(0, h, b)), 0.0)
        by_beta = inv * row(1, h, b)
        tv = jnp.concatenate(split(by_beta), axis=1)
        tk = jnp.concatenate(split(by_beta * (carry_row * n_row)), axis=1)
        vb, kb = v_ref[b * sub : (b + 1) * sub, cols(h)], keys(h, b)
        return jnp.concatenate(
            [mm(tv, jnp.concatenate([vb, vb], axis=0)), mm(tk, jnp.concatenate([kb, kb], axis=0))],
            axis=1,
        )

    writes = over(write, invs, n_rows)

    def block_step(h, b, wrote, n_col, c_col):
        c_end = row(0, h, b)[:, sub - 1 : sub]
        e_col = jnp.where(blocks_geo[b][4], jnp.exp(jnp.minimum(c_end - c_col, 0.0)), 0.0) * n_col
        kb = keys(h, b)
        moved = mm_tn(
            jnp.concatenate([kb, kb], axis=0), jnp.concatenate(split(wrote * e_col), axis=0)
        )
        carry_end = jnp.where(blocks_geo[b][5], jnp.exp(c_end), 0.0)
        return moved[:, :width], carry_end * eye_f - moved[:, width:]

    steps = over(block_step, writes, n_cols, c_cols)

    def read_weights(h, b, n_row):
        qb, c_row = q_ref[b * BLOCK : (b + 1) * BLOCK, cols(h)], row(0, h, b)
        qf = qb.astype(f32)
        nq = lax.rsqrt(jnp.sum(qf * qf, axis=1, keepdims=True) + epsilon) * width ** (-0.5)
        ct = jnp.sum(jnp.where(pick_tok, c_row, 0.0), axis=1, keepdims=True)
        ratio = jnp.where(blocks_geo[b][1], jnp.exp(jnp.minimum(ct - c_row, 0.0)), 0.0)
        carried = (jnp.where(blocks_geo[b][3], jnp.exp(ct), 0.0) * nq) * qf
        return (ratio * mm_nt(qb, keys(h, b)) * nq * n_row).astype(bf16), carried

    weights = over(read_weights, n_rows)

    def read(h, b, weight, wrote):
        got = mm(weight[0], wrote.astype(bf16))
        return got[:, :width], weight[1] - got[:, width:]

    reads = over(read, weights, writes)

    def emit(h, b, own, back):
        oloc_ref[b * BLOCK : (b + 1) * BLOCK, cols(h)] = own
        read_ref[b * BLOCK : (b + 1) * BLOCK, cols(h)] = back.astype(bf16)

    at = lambda h, b: h * blocks + b
    states = [jnp.concatenate(steps[at(h, 0)], axis=1) for h in range(HEADS_STEP)]
    for h in range(HEADS_STEP):
        emit(h, 0, *reads[at(h, 0)])
    for b in range(1, blocks):
        for h in range(HEADS_STEP):
            block_add, block_map = steps[at(h, b)]
            own, back = reads[at(h, b)]
            s_hi, s_lo = split(states[h])
            m_hi, m_lo = split(block_map)
            moved = mm(back.astype(bf16), s_hi)
            emit(h, b, own + moved[:, :width], moved[:, width:])
            grown = mm(
                jnp.concatenate([m_hi, m_lo], axis=1), jnp.concatenate([s_hi, s_hi], axis=0)
            ) + mm(m_hi, s_lo)
            states[h] = jnp.concatenate([grown[:, :width] + block_add, grown[:, width:]], axis=1)
    for h in range(HEADS_STEP):
        add_ref[h] = states[h][:, :width]
        map_ref[h] = states[h][:, width:]


def local_part(lengths, q, k, v, beta, gate):
    tokens, heads = gate.shape
    refl = k.shape[0] // tokens
    width = q.shape[1] // heads
    blocks = tokens // BLOCK
    wide = HEADS_STEP * width
    whole = lambda *shape: pl.BlockSpec(shape, lambda i: (0,) * len(shape))
    column = lambda rows: pl.BlockSpec((rows, wide), lambda i: (0, i))
    square = pl.BlockSpec((HEADS_STEP, width, width), lambda i: (i, 0, 0))
    return pl.pallas_call(
        functools.partial(local_kernel, refl, blocks),
        grid=(heads // HEADS_STEP,),
        in_specs=[
            pl.BlockSpec(memory_space=pltpu.SMEM),
            column(tokens), column(tokens * refl), column(tokens * refl),
            whole(*beta.shape), whole(*gate.shape),
        ],
        out_specs=[column(tokens), column(tokens), square, square],
        out_shape=[
            jax.ShapeDtypeStruct(q.shape, f32),
            jax.ShapeDtypeStruct(q.shape, bf16),
            jax.ShapeDtypeStruct((heads, width, width), f32),
            jax.ShapeDtypeStruct((heads, width, width), f32),
        ],
        scratch_shapes=[pltpu.VMEM((blocks, 2, heads, refl * BLOCK), f32)],
        compiler_params=pltpu.CompilerParams(vmem_limit_bytes=48 * 2**20),
    )(lengths, q, k, v, beta, gate)


def tail_kernel(
    oloc_ref, read_ref, add_ref, map_ref, gain_ref, weight_hbm, out_ref,
    weight_ref, weight_sem, state_in, state_out, normed_ref, own_ref, part_out, part_in,
    state_send, state_recv, part_send, part_recv,
):
    heads, width = add_ref.shape[:2]
    seq_count, head_count = lax.axis_size("seq"), lax.axis_size("head")
    seq_here, head_here = lax.axis_index("seq"), lax.axis_index("head")
    chunk = out_ref.shape[0]
    first, last = seq_here == 0, seq_here == seq_count - 1
    load = pltpu.make_async_copy(weight_hbm, weight_ref, weight_sem)
    load.start()

    barrier = pltpu.get_barrier_semaphore()

    @pl.when(seq_here > 0)
    def _():
        pl.semaphore_signal(barrier, inc=1, device_id={"seq": seq_here - 1}, device_id_type=MESH)

    @pl.when(seq_here < seq_count - 1)
    def _():
        pl.semaphore_signal(barrier, inc=1, device_id={"seq": seq_here + 1}, device_id_type=MESH)

    others = [lax.rem(head_here + d, head_count) for d in range(1, head_count)]
    for other in others:
        pl.semaphore_signal(barrier, inc=1, device_id={"head": other}, device_id_type=MESH)
    expected = jnp.where(first, 0, 1) + jnp.where(last, 0, 1) + head_count - 1
    pl.semaphore_wait(barrier, expected)

    @pl.when(first)
    def _():
        state_in[...] = jnp.zeros_like(state_in)

    def hop(g):
        part = pl.ds(g * STATE_GROUP, STATE_GROUP)
        return pltpu.make_async_remote_copy(
            src_ref=state_out.at[part],
            dst_ref=state_in.at[part],
            send_sem=state_send.at[g],
            recv_sem=state_recv.at[g],
            device_id={"seq": lax.rem(seq_here + 1, seq_count)},
            device_id_type=MESH,
        )

    for g in range(heads // STATE_GROUP):
        @pl.when(seq_here > 0)
        def _():
            hop(g).wait_recv()

        group = range(g * STATE_GROUP, (g + 1) * STATE_GROUP)

        @pl.when(seq_here < seq_count - 1)
        def _():
            for h in group:
                state = state_in[h]
                both = jnp.concatenate(split(map_ref[h]), axis=1)
                grown = add_ref[h] + mm(both, jnp.concatenate([state, state], axis=0))
                state_out[h] = grown.astype(bf16)
            hop(g).start()

        for h in group:
            cols = slice(h * width, (h + 1) * width)
            out = oloc_ref[:, cols] + mm(read_ref[:, cols], state_in[h])
            scale = lax.rsqrt(jnp.mean(out * out, axis=-1, keepdims=True) + epsilon)
            normed_ref[:, cols] = (out * scale * gain_ref[...]).astype(bf16)

    load.wait()
    piece = weight_ref.shape[1] // PIECES
    copies = []
    for slot, other in enumerate(others):
        rows = normed_ref[pl.ds(pl.multiple_of(other * chunk, chunk), chunk), :]
        for p in range(PIECES):
            cols = pl.ds(p * piece, piece)
            part_out[slot, :, cols] = mm(rows, weight_ref[:, cols]).astype(bf16)
            copies.append(
                pltpu.make_async_remote_copy(
                    src_ref=part_out.at[slot, :, cols],
                    dst_ref=part_in.at[slot, :, cols],
                    send_sem=part_send.at[slot, p],
                    recv_sem=part_recv.at[slot, p],
                    device_id={"head": other},
                    device_id_type=MESH,
                )
            )
            copies[-1].start()
    rows = normed_ref[pl.ds(pl.multiple_of(head_here * chunk, chunk), chunk), :]
    for p in range(PIECES):
        cols = pl.ds(p * piece, piece)
        own_ref[:, cols] = mm(rows, weight_ref[:, cols])
    for p in range(PIECES):
        cols = pl.ds(p * piece, piece)
        total = own_ref[:, cols].astype(bf16).astype(f32)
        for slot in range(len(others)):
            copies[slot * PIECES + p].wait_recv()
            total += part_in[slot, :, cols].astype(f32)
        out_ref[:, cols] = total.astype(bf16)
    for copy in copies:
        copy.wait_send()

    @pl.when(seq_here < seq_count - 1)
    def _():
        for g in range(heads // STATE_GROUP):
            hop(g).wait_send()


def tail_part(oloc, read, add, maps, gain, weight):
    tokens, wide = oloc.shape
    heads, width = add.shape[:2]
    head_count = lax.axis_size("head")
    chunk, model = tokens // head_count, weight.shape[1]
    groups = heads // STATE_GROUP
    slots = max(head_count - 1, 1)
    vmem = pl.BlockSpec(memory_space=pltpu.VMEM)
    return pl.pallas_call(
        tail_kernel,
        in_specs=[vmem] * 5 + [pl.BlockSpec(memory_space=pl.ANY)],
        out_specs=vmem,
        out_shape=jax.ShapeDtypeStruct((chunk, model), bf16),
        scratch_shapes=[
            pltpu.VMEM(weight.shape, bf16),
            pltpu.SemaphoreType.DMA,
            pltpu.VMEM((heads, width, width), bf16),
            pltpu.VMEM((heads, width, width), bf16),
            pltpu.VMEM((tokens, wide), bf16),
            pltpu.VMEM((chunk, model), f32),
            pltpu.VMEM((slots, chunk, model), bf16),
            pltpu.VMEM((slots, chunk, model), bf16),
            pltpu.SemaphoreType.DMA((groups,)),
            pltpu.SemaphoreType.DMA((groups,)),
            pltpu.SemaphoreType.DMA((slots, PIECES)),
            pltpu.SemaphoreType.DMA((slots, PIECES)),
        ],
        compiler_params=pltpu.CompilerParams(
            collective_id=0, has_side_effects=True, vmem_limit_bytes=32 * 2**20
        ),
    )(oloc, read, add, maps, gain, weight)


def body(queries, reflect_keys, reflect_values, reflect_beta, log_decay, prompt_lengths, norm_gain, out_weight):
    tokens, refl, wide = reflect_keys.shape[1:]
    heads = log_decay.shape[2]
    oloc, read, add, maps = local_part(
        prompt_lengths,
        queries[0],
        reflect_keys[0].reshape(tokens * refl, wide),
        reflect_values[0].reshape(tokens * refl, wide),
        reflect_beta[0].reshape(tokens, refl * heads),
        log_decay[0],
    )
    return tail_part(oloc, read, add, maps, norm_gain[None], out_weight)[None]


def solution(mesh):
    in_specs = (
        P(("parts", "rep"), "seq", "head"),
        P(("parts", "rep"), "seq", None, "head"),
        P(("parts", "rep"), "seq", None, "head"),
        P(("parts", "rep"), "seq", None, "head"),
        P(("parts", "rep"), "seq", "head"),
        P(("parts", "rep"), None),
        P(),
        P("head", None),
    )
    out_specs = P(("parts", "rep"), ("seq", "head"), None)
    return jax.shard_map(body, mesh=mesh, in_specs=in_specs, out_specs=out_specs, check_vma=False)
```

time: 142 us -> 48.6 us (0.34); the launches traced: 140 us -> 48.4 us
  waiting for transfers between devices: 44.5 us -> 0 us
  Pallas kernels: 67.8 us -> 40.6 us
  between operations: 13.6 us -> 0.08 us
  matrix products: 4.28 us -> 0 us
  starting transfers between devices: 3.88 us -> 0 us
  local copies, waits for them, and re-layouts: 5.98 us -> 7.62 us
    pallas_call x1, Pallas kernels: 67.8 us -> 13.5 us  [local_part(): pl.pallas_call(functools.partial(local_kernel, refl, blocks), grid=(heads...]
    pallas_call x0 -> x1, Pallas kernels: none -> 27.2 us  [tail_part(): pl.pallas_call(tail_kernel, in_specs=[vmem] * 5 + [pl.BlockSpec(memory_sp...]
    ppermute x3 -> x0, waiting for transfers between devices: 23 us -> none  [body(): lax.ppermute(grown.astype(bf16), 'seq', [(s, s + 1) for s in range(count...]
    reduce_scatter x1 -> x0, waiting for transfers between devices: 21.5 us -> none  [body(): lax.psum_scatter(partial, 'head', scatter_dimension=0, tiled=True)[None]]
    dot_general x5 -> x0, matrix products: 4.28 us -> none  [the longest x1 2.24 us: body(): jnp.dot(normed.reshape(tokens, wide), out_weight, preferred_element_type=...]
    ppermute x3 -> x0, starting transfers between devices: 3.88 us -> none  [body(): lax.ppermute(grown.astype(bf16), 'seq', [(s, s + 1) for s in range(count...]
    unnamed x11 -> x10, local copies, waits for them, and re-layouts: 1.88 us -> 3.81 us
  transfers between devices with their start and end apart: 4 -> 0, of which waited for: 4 -> 0; matrix products, arithmetic and copies ran while one was open for 0% -> 0% of each run, Pallas kernels for 0% -> 0%
where the time goes in v1:
time: 48.6 us; the launch traced here: 48.4 us
  Pallas kernels  40.6 us (84%)
  local copies, waits for them, and re-layouts  7.62 us (16%)
    pallas_call x1, Pallas kernels, tail_part(): pl.pallas_call(tail_kernel, in_specs=[vmem] * 5 + [pl.BlockSpec(memory_sp...  27.2 us
    pallas_call x1, Pallas kernels, local_part(): pl.pallas_call(functools.partial(local_kernel, refl, blocks), grid=(heads...  13.5 us
    unnamed x10, local copies, waits for them, and re-layouts  3.81 us
    another operation x1, local copies, waits for them, and re-layouts, body(): reflect_keys[0].reshape(tokens * refl, wide)  1.47 us
    another operation x1, local copies, waits for them, and re-layouts, body(): reflect_values[0].reshape(tokens * refl, wide)  1.47 us

profile of v1, /device:TPU:28, one launch (start us, length us, event | category | flops | bytes accessed | tf_op | source)
XLA Modules:
  0.0 48.4 jit_solution(7585664509664553299)
XLA Ops:
  0.0 0.0 copy-start.3
  0.0 0.0 copy-start.2
  0.0 0.0 copy-start.1
  0.0 0.9 %copy.12.beta_ref = f32[256,16]{1,0:T(8,128)S(1)} copy(f32[256,16]{0,1:T(8,128)} %bitcast.9) | data formatting | bytes 32768 | tf_op jit(solution)/shard_map/reshape;squeeze | solution.py:408
  0.9 0.8 %copy.11 = f32[1,256,8]{2,1,0:T(8,128)S(1)} copy(f32[1,256,8]{1,2,0:T(8,128)} %param.12) | data formatting | bytes 16384 | tf_op args[4]
  1.7 1.5 %reshape_squeeze.9.k_ref = bf16[512,1024]{1,0:T(8,128)(2,1)S(1)} reshape(bf16[1,256,2,1024]{3,2,1,0:T(2,128)(2,1)} %param.9) | data formatting | bytes 2097152 | tf_op jit(solution)/shard_map/reshape;squeeze | solution.py:406
  3.2 1.5 %reshape_squeeze.10.v_ref = bf16[512,1024]{1,0:T(8,128)(2,1)S(1)} reshape(bf16[1,256,2,1024]{3,2,1,0:T(2,128)(2,1)} %param.10) | data formatting | bytes 2097152 | tf_op jit(solution)/shard_map/reshape;squeeze | solution.py:407
  4.7 0.0 copy-done.2
  4.7 0.0 copy-done.1
  4.7 13.5 %shard_map.82 = (f32[256,1024]{1,0:T(8,128)S(1)}, bf16[256,1024]{1,0:T(8,128)(2,1)S(1)}, f32[8,128,128]{2,1,0:T(8,128)S(1)}, f32[8,128,128]{2,1,0:T(8,128)S(1)}) custom-call(s32[1,6]{1,0:T(1,128)S(1)} %copy-done.2, bf16[256,1024]{1,0:T(8,128)(2,1)S(1)} %bitcast.7, bf16[512,1024]{1,0:T(8,128)(2,1)S(1)} %reshape_squeeze.9.k_ref, ...), custom_call_target="tpu_custom_call" | custom-call | tf_op jit(solution)/shard_map/pallas_call | solution.py:242
  18.2 0.0 copy-done.3
  18.2 0.0 copy-start
  18.2 2.2 %copy-done = bf16[1024,2048]{1,0:T(8,128)(2,1)S(1)} copy-done((bf16[1024,2048]{1,0:T(8,128)(2,1)S(1)}, bf16[1024,2048]{1,0:T(8,128)(2,1)}, u32[]{:S(2)}) %copy-start) | copy-done | bytes 4194328
  20.4 27.2 %shard_map.83 = bf16[128,2048]{1,0:T(8,128)(2,1)S(1)} custom-call(f32[256,1024]{1,0:T(8,128)S(1)} %get-tuple-element.9.oloc_ref, bf16[256,1024]{1,0:T(8,128)(2,1)S(1)} %get-tuple-element.10.read_ref, f32[8,128,128]{2,1,0:T(8,128)S(1)} %get-tuple-element.11.add_ref, f32[8,128,128]{2,1,0:T(8,128)S(1)} %get-tuple-element.12.map_ref, f32[1,128]{1,0:T(1,128)S(1)} %bitcast.8, ...), custom_call_target="tpu_custom_call" | custom-call | tf_op jit(solution)/shard_map/pallas_call | solution.py:375
  47.6 0.8 %copy.14 = bf16[1,128,2048]{2,1,0:T(8,128)(2,1)} copy(bf16[1,128,2048]{2,1,0:T(8,128)(2,1)S(1)} %bitcast.5) | data formatting | bytes 1048576
Async XLA Ops:
  0.0 18.2 %copy-start.3 = (f32[128]{0:T(128)S(1)}, f32[128]{0:T(128)}, u32[]{:S(2)}) copy-start(f32[128]{0:T(128)} %param.14) | copy-start | bytes 1540
  0.0 4.7 %copy-start.2 = (s32[1,6]{1,0:T(1,128)S(1)}, s32[1,6]{1,0:T(1,128)}, u32[]{:S(2)}) copy-start(s32[1,6]{1,0:T(1,128)} %len_ref.1) | copy-start | bytes 76
  0.0 4.7 %copy-start.1 = (bf16[1,256,1024]{2,1,0:T(8,128)(2,1)S(1)}, bf16[1,256,1024]{2,1,0:T(8,128)(2,1)}, u32[]{:S(2)}) copy-start(bf16[1,256,1024]{2,1,0:T(8,128)(2,1)} %param.8) | copy-start | bytes 1572868
  18.2 2.2 %copy-start = (bf16[1024,2048]{1,0:T(8,128)(2,1)S(1)}, bf16[1024,2048]{1,0:T(8,128)(2,1)}, u32[]{:S(2)}) copy-start(bf16[1024,2048]{1,0:T(8,128)(2,1)} %weight_hbm.1) | copy-start | bytes 12582916

commit v2 on v1

--- a/solution.py
+++ b/solution.py
@@ -19,18 +19,16 @@
 highest = lax.Precision.HIGHEST
 
 
-def mm(a, b):
-    return jnp.dot(a, b, preferred_element_type=f32)
+def mm(a, b, precision=None):
+    return jnp.dot(a, b, preferred_element_type=f32, precision=precision)
 
 
 def mm_nt(a, b):
     return lax.dot_general(a, b, (((1,), (1,)), ((), ())), preferred_element_type=f32)
 
 
-def mm_tn(a, b, precision=None):
-    return lax.dot_general(
-        a, b, (((0,), (0,)), ((), ())), preferred_element_type=f32, precision=precision
-    )
+def mm_tn(a, b):
+    return lax.dot_general(a, b, (((0,), (0,)), ((), ())), preferred_element_type=f32)
 
 
 def split(x):
@@ -44,7 +42,7 @@
 ):
     sub = refl * BLOCK
     width = k_ref.shape[1] // HEADS_STEP
-    heads = gate_ref.shape[1]
+    heads = gate_ref.shape[0]
     tokens = blocks * BLOCK
     step = pl.program_id(0)
 
@@ -55,12 +53,12 @@
         for b in range(blocks):
             rel = tok - b * BLOCK
             cum = jnp.where((rel >= 0) & (rel <= lane // refl), 1.0, 0.0).astype(f32)
-            rows_ref[b, 0] = mm_tn(gate_ref[...], cum, highest)
+            rows_ref[b, 0] = mm(gate_ref[...], cum, highest)
             total = jnp.zeros((heads, sub), f32)
             for j in range(refl):
                 pick = jnp.where(rel * refl + j == lane, 1.0, 0.0).astype(f32)
                 pick = jnp.where(rel >= 0, pick, 0.0)
-                total += mm_tn(beta_ref[:, j * heads : (j + 1) * heads], pick, highest)
+                total += mm(beta_ref[j], pick, highest)
             rows_ref[b, 1] = total
 
     offset = lax.axis_index("seq") * tokens
@@ -206,8 +204,8 @@
     reads = over(read, weights, writes)
 
     def emit(h, b, own, back):
-        oloc_ref[b * BLOCK : (b + 1) * BLOCK, cols(h)] = own
-        read_ref[b * BLOCK : (b + 1) * BLOCK, cols(h)] = back.astype(bf16)
+        oloc_ref[step, b * BLOCK : (b + 1) * BLOCK, cols(h)] = own
+        read_ref[step, b * BLOCK : (b + 1) * BLOCK, cols(h)] = back.astype(bf16)
 
     at = lambda h, b: h * blocks + b
     states = [jnp.concatenate(steps[at(h, 0)], axis=1) for h in range(HEADS_STEP)]
@@ -226,71 +224,55 @@
             ) + mm(m_hi, s_lo)
             states[h] = jnp.concatenate([grown[:, :width] + block_add, grown[:, width:]], axis=1)
     for h in range(HEADS_STEP):
-        add_ref[h] = states[h][:, :width]
-        map_ref[h] = states[h][:, width:]
-
-
-def local_part(lengths, q, k, v, beta, gate):
-    tokens, heads = gate.shape
-    refl = k.shape[0] // tokens
-    width = q.shape[1] // heads
-    blocks = tokens // BLOCK
-    wide = HEADS_STEP * width
-    whole = lambda *shape: pl.BlockSpec(shape, lambda i: (0,) * len(shape))
-    column = lambda rows: pl.BlockSpec((rows, wide), lambda i: (0, i))
-    square = pl.BlockSpec((HEADS_STEP, width, width), lambda i: (i, 0, 0))
-    return pl.pallas_call(
-        functools.partial(local_kernel, refl, blocks),
-        grid=(heads // HEADS_STEP,),
-        in_specs=[
-            pl.BlockSpec(memory_space=pltpu.SMEM),
-            column(tokens), column(tokens * refl), column(tokens * refl),
-            whole(*beta.shape), whole(*gate.shape),
-        ],
-        out_specs=[column(tokens), column(tokens), square, square],
-        out_shape=[
-            jax.ShapeDtypeStruct(q.shape, f32),
-            jax.ShapeDtypeStruct(q.shape, bf16),
-            jax.ShapeDtypeStruct((heads, width, width), f32),
-            jax.ShapeDtypeStruct((heads, width, width), f32),
-        ],
-        scratch_shapes=[pltpu.VMEM((blocks, 2, heads, refl * BLOCK), f32)],
-        compiler_params=pltpu.CompilerParams(vmem_limit_bytes=48 * 2**20),
-    )(lengths, q, k, v, beta, gate)
-
-
-def tail_kernel(
-    oloc_ref, read_ref, add_ref, map_ref, gain_ref, weight_hbm, out_ref,
+        add_ref[step * HEADS_STEP + h] = states[h][:, :width]
+        map_ref[step * HEADS_STEP + h] = states[h][:, width:]
+
+
+def mixer_kernel(
+    refl, blocks, len_ref, q_ref, k_ref, v_ref, beta_ref, gate_ref, gain_ref, weight_hbm, out_ref,
+    rows_ref, oloc_ref, read_ref, add_ref, map_ref,
     weight_ref, weight_sem, state_in, state_out, normed_ref, own_ref, part_out, part_in,
     state_send, state_recv, part_send, part_recv,
 ):
     heads, width = add_ref.shape[:2]
+    step, steps = pl.program_id(0), heads // HEADS_STEP
+    groups = heads // STATE_GROUP
     seq_count, head_count = lax.axis_size("seq"), lax.axis_size("head")
     seq_here, head_here = lax.axis_index("seq"), lax.axis_index("head")
     chunk = out_ref.shape[0]
     first, last = seq_here == 0, seq_here == seq_count - 1
+    others = [lax.rem(head_here + d, head_count) for d in range(1, head_count)]
     load = pltpu.make_async_copy(weight_hbm, weight_ref, weight_sem)
-    load.start()
-
-    barrier = pltpu.get_barrier_semaphore()
-
-    @pl.when(seq_here > 0)
+
+    @pl.when(step == 0)
     def _():
-        pl.semaphore_signal(barrier, inc=1, device_id={"seq": seq_here - 1}, device_id_type=MESH)
-
-    @pl.when(seq_here < seq_count - 1)
+        load.start()
+        barrier = pltpu.get_barrier_semaphore()
+
+        @pl.when(seq_here > 0)
+        def _():
+            pl.semaphore_signal(barrier, inc=1, device_id={"seq": seq_here - 1}, device_id_type=MESH)
+
+        @pl.when(seq_here < seq_count - 1)
+        def _():
+            pl.semaphore_signal(barrier, inc=1, device_id={"seq": seq_here + 1}, device_id_type=MESH)
+
+        for other in others:
+            pl.semaphore_signal(barrier, inc=1, device_id={"head": other}, device_id_type=MESH)
+
+    local_kernel(
+        refl, blocks, len_ref, q_ref, k_ref, v_ref, beta_ref, gate_ref,
+        oloc_ref, read_ref, add_ref, map_ref, rows_ref,
+    )
+
+    @pl.when(step == 0)
     def _():
-        pl.semaphore_signal(barrier, inc=1, device_id={"seq": seq_here + 1}, device_id_type=MESH)
-
-    others = [lax.rem(head_here + d, head_count) for d in range(1, head_count)]
-    for other in others:
-        pl.semaphore_signal(barrier, inc=1, device_id={"head": other}, device_id_type=MESH)
-    expected = jnp.where(first, 0, 1) + jnp.where(last, 0, 1) + head_count - 1
-    pl.semaphore_wait(barrier, expected)
-
-    @pl.when(first)
-    def _():
-        state_in[...] = jnp.zeros_like(state_in)
+        expected = jnp.where(first, 0, 1) + jnp.where(last, 0, 1) + head_count - 1
+        pl.semaphore_wait(pltpu.get_barrier_semaphore(), expected)
+
+        @pl.when(first)
+        def _():
+            state_in[...] = jnp.zeros_like(state_in)
 
     def hop(g):
         part = pl.ds(g * STATE_GROUP, STATE_GROUP)
@@ -303,112 +285,132 @@
             device_id_type=MESH,
         )
 
-    for g in range(heads // STATE_GROUP):
-        @pl.when(seq_here > 0)
-        def _():
-            hop(g).wait_recv()
-
-        group = range(g * STATE_GROUP, (g + 1) * STATE_GROUP)
+    @pl.when((seq_here == 0) & (seq_here < seq_count - 1))
+    def _():
+        for g in range(HEADS_STEP // STATE_GROUP):
+            here = step * (HEADS_STEP // STATE_GROUP) + g
+            for h in range(STATE_GROUP):
+                state_out[here * STATE_GROUP + h] = add_ref[here * STATE_GROUP + h].astype(bf16)
+            hop(here).start()
+
+    @pl.when(step == steps - 1)
+    def _():
+        for g in range(groups):
+            group = range(g * STATE_GROUP, (g + 1) * STATE_GROUP)
+
+            @pl.when(seq_here > 0)
+            def _():
+                hop(g).wait_recv()
+
+            @pl.when((seq_here > 0) & (seq_here < seq_count - 1))
+            def _():
+                for h in group:
+                    state = state_in[h]
+                    both = jnp.concatenate(split(map_ref[h]), axis=1)
+                    grown = add_ref[h] + mm(both, jnp.concatenate([state, state], axis=0))
+                    state_out[h] = grown.astype(bf16)
+                hop(g).start()
+
+            for h in group:
+                cols = slice(h * width, (h + 1) * width)
+                at, local = h // HEADS_STEP, slice(h % HEADS_STEP * width, (h % HEADS_STEP + 1) * width)
+                out = oloc_ref[at, :, local] + mm(read_ref[at, :, local], state_in[h])
+                scale = lax.rsqrt(jnp.mean(out * out, axis=-1, keepdims=True) + epsilon)
+                normed_ref[:, cols] = (out * scale * gain_ref[...]).astype(bf16)
+
+        load.wait()
+        piece = weight_ref.shape[1] // PIECES
+        copies = []
+        for slot, other in enumerate(others):
+            rows = normed_ref[pl.ds(pl.multiple_of(other * chunk, chunk), chunk), :]
+            for p in range(PIECES):
+                cols = pl.ds(p * piece, piece)
+                part_out[slot, :, cols] = mm(rows, weight_ref[:, cols]).astype(bf16)
+                copies.append(
+                    pltpu.make_async_remote_copy(
+                        src_ref=part_out.at[slot, :, cols],
+                        dst_ref=part_in.at[slot, :, cols],
+                        send_sem=part_send.at[slot, p],
+                        recv_sem=part_recv.at[slot, p],
+                        device_id={"head": other},
+                        device_id_type=MESH,
+                    )
+                )
+                copies[-1].start()
+        rows = normed_ref[pl.ds(pl.multiple_of(head_here * chunk, chunk), chunk), :]
+        for p in range(PIECES):
+            cols = pl.ds(p * piece, piece)
+            own_ref[:, cols] = mm(rows, weight_ref[:, cols])
+        for p in range(PIECES):
+            cols = pl.ds(p * piece, piece)
+            total = own_ref[:, cols].astype(bf16).astype(f32)
+            for slot in range(len(others)):
+                copies[slot * PIECES + p].wait_recv()
+                total += part_in[slot, :, cols].astype(f32)
+            out_ref[:, cols] = total.astype(bf16)
+        for copy in copies:
+            copy.wait_send()
 
         @pl.when(seq_here < seq_count - 1)
         def _():
-            for h in group:
-                state = state_in[h]
-                both = jnp.concatenate(split(map_ref[h]), axis=1)
-                grown = add_ref[h] + mm(both, jnp.concatenate([state, state], axis=0))
-                state_out[h] = grown.astype(bf16)
-            hop(g).start()
-
-        for h in group:
-            cols = slice(h * width, (h + 1) * width)
-            out = oloc_ref[:, cols] + mm(read_ref[:, cols], state_in[h])
-            scale = lax.rsqrt(jnp.mean(out * out, axis=-1, keepdims=True) + epsilon)
-            normed_ref[:, cols] = (out * scale * gain_ref[...]).astype(bf16)
-
-    load.wait()
-    piece = weight_ref.shape[1] // PIECES
-    copies = []
-    for slot, other in enumerate(others):
-        rows = normed_ref[pl.ds(pl.multiple_of(other * chunk, chunk), chunk), :]
-        for p in range(PIECES):
-            cols = pl.ds(p * piece, piece)
-            part_out[slot, :, cols] = mm(rows, weight_ref[:, cols]).astype(bf16)
-            copies.append(
-                pltpu.make_async_remote_copy(
-                    src_ref=part_out.at[slot, :, cols],
-                    dst_ref=part_in.at[slot, :, cols],
-                    send_sem=part_send.at[slot, p],
-                    recv_sem=part_recv.at[slot, p],
-                    device_id={"head": other},
-                    device_id_type=MESH,
-                )
-            )
-            copies[-1].start()
-    rows = normed_ref[pl.ds(pl.multiple_of(head_here * chunk, chunk), chunk), :]
-    for p in range(PIECES):
-        cols = pl.ds(p * piece, piece)
-        own_ref[:, cols] = mm(rows, weight_ref[:, cols])
-    for p in range(PIECES):
-        cols = pl.ds(p * piece, piece)
-        total = own_ref[:, cols].astype(bf16).astype(f32)
-        for slot in range(len(others)):
-            copies[slot * PIECES + p].wait_recv()
-            total += part_in[slot, :, cols].astype(f32)
-        out_ref[:, cols] = total.astype(bf16)
-    for copy in copies:
-        copy.wait_send()
-
-    @pl.when(seq_here < seq_count - 1)
-    def _():
-        for g in range(heads // STATE_GROUP):
-            hop(g).wait_send()
-
-
-def tail_part(oloc, read, add, maps, gain, weight):
-    tokens, wide = oloc.shape
-    heads, width = add.shape[:2]
+            for g in range(groups):
+                hop(g).wait_send()
+
+
+def body(queries, reflect_keys, reflect_values, reflect_beta, log_decay, prompt_lengths, norm_gain, out_weight):
+    tokens, refl, wide = reflect_keys.shape[1:]
+    heads = log_decay.shape[2]
+    width = wide // heads
+    blocks = tokens // BLOCK
     head_count = lax.axis_size("head")
-    chunk, model = tokens // head_count, weight.shape[1]
-    groups = heads // STATE_GROUP
-    slots = max(head_count - 1, 1)
-    vmem = pl.BlockSpec(memory_space=pltpu.VMEM)
-    return pl.pallas_call(
-        tail_kernel,
-        in_specs=[vmem] * 5 + [pl.BlockSpec(memory_space=pl.ANY)],
-        out_specs=vmem,
+    chunk, model = tokens // head_count, out_weight.shape[1]
+    groups, steps, slots = heads // STATE_GROUP, heads // HEADS_STEP, max(head_count - 1, 1)
+    wide_step = HEADS_STEP * width
+    beta, gate = reflect_beta[0].transpose(1, 2, 0), log_decay[0].T
+    whole = lambda shape: pl.BlockSpec(shape, lambda i: (0,) * len(shape))
+    column = lambda rows: pl.BlockSpec((rows, wide_step), lambda i: (0, i))
+    dma = pltpu.SemaphoreType.DMA
+    out = pl.pallas_call(
+        functools.partial(mixer_kernel, refl, blocks),
+        grid=(steps,),
+        in_specs=[
+            pl.BlockSpec(memory_space=pltpu.SMEM),
+            column(tokens), column(tokens * refl), column(tokens * refl),
+            whole(beta.shape), whole(gate.shape), whole((1, width)),
+            pl.BlockSpec(memory_space=pl.ANY),
+        ],
+        out_specs=whole((chunk, model)),
         out_shape=jax.ShapeDtypeStruct((chunk, model), bf16),
         scratch_shapes=[
-            pltpu.VMEM(weight.shape, bf16),
-            pltpu.SemaphoreType.DMA,
+            pltpu.VMEM((blocks, 2, heads, refl * BLOCK), f32),
+            pltpu.VMEM((steps, tokens, wide_step), f32),
+            pltpu.VMEM((steps, tokens, wide_step), bf16),
+            pltpu.VMEM((heads, width, width), f32),
+            pltpu.VMEM((heads, width, width), f32),
+            pltpu.VMEM(out_weight.shape, bf16),
+            dma,
             pltpu.VMEM((heads, width, width), bf16),
             pltpu.VMEM((heads, width, width), bf16),
             pltpu.VMEM((tokens, wide), bf16),
             pltpu.VMEM((chunk, model), f32),
             pltpu.VMEM((slots, chunk, model), bf16),
             pltpu.VMEM((slots, chunk, model), bf16),
-            pltpu.SemaphoreType.DMA((groups,)),
-            pltpu.SemaphoreType.DMA((groups,)),
-            pltpu.SemaphoreType.DMA((slots, PIECES)),
-            pltpu.SemaphoreType.DMA((slots, PIECES)),
+            dma((groups,)), dma((groups,)), dma((slots, PIECES)), dma((slots, PIECES)),
         ],
         compiler_params=pltpu.CompilerParams(
-            collective_id=0, has_side_effects=True, vmem_limit_bytes=32 * 2**20
+            collective_id=0, has_side_effects=True, vmem_limit_bytes=56 * 2**20
         ),
-    )(oloc, read, add, maps, gain, weight)
-
-
-def body(queries, reflect_keys, reflect_values, reflect_beta, log_decay, prompt_lengths, norm_gain, out_weight):
-    tokens, refl, wide = reflect_keys.shape[1:]
-    heads = log_decay.shape[2]
-    oloc, read, add, maps = local_part(
+    )(
         prompt_lengths,
         queries[0],
         reflect_keys[0].reshape(tokens * refl, wide),
         reflect_values[0].reshape(tokens * refl, wide),
-        reflect_beta[0].reshape(tokens, refl * heads),
-        log_decay[0],
+        beta,
+        gate,
+        norm_gain[None],
+        out_weight,
     )
-    return tail_part(oloc, read, add, maps, norm_gain[None], out_weight)[None]
+    return out[None]
 
 
 def solution(mesh):

time: 48.6 us -> 44.4 us (0.914)
  Pallas kernels: 40.6 us -> 37.8 us
  local copies, waits for them, and re-layouts: 7.62 us -> 6.42 us
    pallas_call x2 -> x1, Pallas kernels: 40.6 us -> 37.8 us  [body(): pl.pallas_call(functools.partial(mixer_kernel, refl, blocks), grid=(steps...]
    unnamed x10 -> x1, local copies, waits for them, and re-layouts: 3.81 us -> 1.88 us
    another operation x1 -> x0, local copies, waits for them, and re-layouts: 0.88 us -> none  [body(): reflect_beta[0].reshape(tokens, refl * heads)]
    another operation x1, local copies, waits for them, and re-layouts: 1.47 us -> 2.28 us  [body(): reflect_values[0].reshape(tokens * refl, wide)]
    another operation x1, local copies, waits for them, and re-layouts: 1.47 us -> 2.26 us  [body(): reflect_keys[0].reshape(tokens * refl, wide)]
where the time goes in v2:
time: 44.4 us; the launch traced here: 44.2 us
  Pallas kernels  37.8 us (85%)
  local copies, waits for them, and re-layouts  6.42 us (14%)
    pallas_call x1, Pallas kernels, body(): pl.pallas_call(functools.partial(mixer_kernel, refl, blocks), grid=(steps...  37.8 us
    another operation x1, local copies, waits for them, and re-layouts, body(): reflect_values[0].reshape(tokens * refl, wide)  2.28 us
    another operation x1, local copies, waits for them, and re-layouts, body(): reflect_keys[0].reshape(tokens * refl, wide)  2.26 us
    unnamed x1, local copies, waits for them, and re-layouts  1.88 us

profile of v2, /device:TPU:28, one launch (start us, length us, event | category | flops | bytes accessed | tf_op | source)
XLA Modules:
  0.0 44.2 jit_solution(1338025293857002409)
XLA Ops:
  0.0 2.3 %reshape_squeeze.6.k_ref = bf16[512,1024]{1,0:T(8,128)(2,1)} reshape(bf16[1,256,2,1024]{3,2,1,0:T(2,128)(2,1)} %param.9) | data formatting | bytes 2097152 | tf_op jit(solution)/shard_map/reshape;squeeze | solution.py:406
  2.3 2.3 %reshape_squeeze.7.v_ref = bf16[512,1024]{1,0:T(8,128)(2,1)} reshape(bf16[1,256,2,1024]{3,2,1,0:T(2,128)(2,1)} %param.10) | data formatting | bytes 2097152 | tf_op jit(solution)/shard_map/reshape;squeeze | solution.py:407
  4.5 37.8 %shard_map.82 = bf16[128,2048]{1,0:T(8,128)(2,1)} custom-call(s32[1,6]{1,0:T(1,128)} %len_ref.1, bf16[256,1024]{1,0:T(8,128)(2,1)} %bitcast.10, bf16[512,1024]{1,0:T(8,128)(2,1)} %reshape_squeeze.6.k_ref, bf16[512,1024]{1,0:T(8,128)(2,1)} %reshape_squeeze.7.v_ref, f32[2,8,256]{2,1,0:T(8,128)} %bitcast.11, f32[8,256]{1,0:T(8,128)} %bitcast.12, ...), custom_call_target="tpu_custom_call" | custom-call | tf_op jit(solution)/shard_map/pallas_call | solution.py:373
  42.3 1.9 %copy.10 = bf16[1,128,2048]{2,1,0:T(8,128)(2,1)} copy(bf16[1,128,2048]{2,1,0:T(8,128)(2,1)} %bitcast.9) | data formatting | bytes 1048576
